TPU v7x, 256 devices: a 4x2x16 block of a 4x16x16 slice. The times are simulated.
256 devices in a mesh: groups: 2 (over y), pool: 64 (over z, x), heads: 2 (over core).
Axes of the slice: x: 4, y: 2, z: 16, core: 2. Of those that a mesh axis runs over, the one named last changes fastest.
The devices are a block of a 4x16x16 slice.
Arguments:
- hidden_in: bfloat16 [32, 8192], P('groups'), parts along dimension 0, may hold values from -50 to 50
- key_cache: bfloat16 [32, 8, 4096, 128], P('groups', 'heads', 'pool'), parts along dimension 0, may hold values from -200 to 200
- value_cache: bfloat16 [32, 8, 4096, 128], P('groups', 'heads', 'pool'), parts along dimension 0, may hold values from -6 to 6
- positions: int32 [3, 32, 4096], P(None, 'groups', 'pool'), parts along dimension 1, may hold values from 0 to 4095, as said below
- query_pos: int32 [3, 32], P(None, 'groups'), parts along dimension 1, may hold values from 4096 to 8207
- lengths: int32 [32], P('groups'), parts along dimension 0, may hold values from 1024 to 4096, as said below
- query_weight: bfloat16 [8192, 8192], P('pool', 'heads'), may hold values from -0.0625 to 0.0625
- key_weight: bfloat16 [8192, 1024], P('pool', 'heads'), may hold values from -0.16503906 to 0.16503906
- value_weight: bfloat16 [8192, 1024], P('pool', 'heads'), may hold values from -0.16503906 to 0.16503906
- out_weight: bfloat16 [8192, 8192], P('heads', 'pool'), may hold values from -0.5 to 0.5
- gate_weight: bfloat16 [8192, 14848], P(None, ('pool', 'heads')), may hold values from -0.0625 to 0.0625
- up_weight: bfloat16 [8192, 14848], P(None, ('pool', 'heads')), may hold values from -0.0625 to 0.0625
- down_weight: bfloat16 [14848, 8192], P(('pool', 'heads')), may hold values from -0.1875 to 0.1875
Outputs:
- output: bfloat16 [32, 8192], P('groups', 'pool'), parts along dimension 0
There are 2 independent parts, one for each index of `groups`. A program takes and returns all parts, laid end to end along the dimension named above; an argument that names none is the same for every part. Nothing has to cross between parts.
Inputs may be any that keep to these rules, and one draw needn't show every extreme that they name: `positions`: text tokens carry three equal ids; one prompt is text only. `lengths`: some prompt fills all 4096 slots.
All inputs are finite; a program needn't handle non-finite values.
Results may differ from a plain program's by a relative error of at most 0.007.
The roundings to bfloat16 on the way count: a program that leaves them out, or rounds other values in their place, can miss the bound.
Values may be sent and summed in bfloat16 or wider, within the bound.
A program may use at most 64 MiB of HBM per device.

v0:
```python
import math

import jax
import jax.numpy as jnp
from jax import lax
from jax.sharding import PartitionSpec as P

D = 8192
HEADS = 64
KV_HEADS = 8
HD = 128
PROMPTS = 16


EPS = 1e-06
THETA = 1000000.0


def split_up(value, dim, size):
    before, after = (value.shape[:dim], value.shape[dim + 1 :])
    return jnp.moveaxis(value.reshape(*before, size, -1, *after), dim, 0)


def sum_at_owner(value, axis, dim):
    size = lax.axis_size(axis)
    pieces = lax.all_to_all(split_up(value, dim, size), axis, 0, 0, tiled=True)
    return jnp.sum(pieces, axis=0)


def sent_together(arrays, axis, split_dim, concat_dim, along):
    ends, at = ([], 0)
    for a in arrays[:-1]:
        at += a.shape[along]
        ends.append(at)
    both = jnp.concatenate(arrays, axis=along)
    return tuple(
        jnp.split(
            lax.all_to_all(both, axis, split_axis=split_dim, concat_axis=concat_dim, tiled=True),
            ends,
            axis=along,
        )
    )


def joined_along(pieces, dim):
    pieces = jnp.moveaxis(pieces, 0, dim)
    lengths = pieces.shape
    return pieces.reshape(*lengths[:dim], lengths[dim] * lengths[dim + 1], *lengths[dim + 2 :])


def copy_for_each(value, axis):
    size = lax.axis_size(axis)
    return lax.all_to_all(
        jnp.broadcast_to(value[None], (size, *value.shape)), axis, 0, 0, tiled=True
    )


def gather_directly(value, axis, dim):
    return joined_along(copy_for_each(value, axis), dim)


def taken_together(value, axis):
    return copy_for_each(value, axis).sum(axis=0)


def sent_and_summed(value, axis, dim):
    pieces = split_up(value, dim, lax.axis_size(axis))
    arrived = lax.all_to_all(pieces, axis, split_axis=0, concat_axis=0, tiled=True)
    return arrived.astype(jnp.float32).sum(axis=0)


def angle_tables(triple):
    half_dim = HD // 2
    column = jnp.arange(half_dim)
    first_end = HD // 8
    second_end = first_end + 3 * HD // 16
    chosen = jnp.where(
        column < first_end,
        triple[0][..., None],
        jnp.where(column < second_end, triple[1][..., None], triple[2][..., None]),
    )
    inverse = jnp.exp(column.astype(jnp.float32) * (-2.0 * math.log(THETA) / HD))
    angles = chosen.astype(jnp.float32) * inverse
    return (jnp.cos(angles), jnp.sin(angles))


def rotate(values, cos_table, sin_table):
    half_dim = values.shape[-1] // 2
    lower_half = values[..., :half_dim]
    upper_half = values[..., half_dim:]
    return jnp.concatenate(
        [
            lower_half * cos_table - upper_half * sin_table,
            upper_half * cos_table + lower_half * sin_table,
        ],
        -1,
    )


def normalize(values):
    return values * lax.rsqrt(jnp.mean(values * values, -1, keepdims=True) + EPS)


def prepare(projected_rows, item_ids, local_heads, query_pos):
    query_width = projected_rows.shape[1] - 2 * HD
    prompt_ids = item_ids // local_heads
    triple = query_pos[:, prompt_ids]
    cos_table, sin_table = angle_tables(triple)
    item_count = projected_rows.shape[0]
    raw_queries = projected_rows[:, :query_width].reshape(item_count, query_width // HD, HD)
    queries = rotate(raw_queries, cos_table[:, None], sin_table[:, None]).astype(jnp.bfloat16)
    own_keys = rotate(
        projected_rows[:, query_width : query_width + HD], cos_table, sin_table
    ).astype(jnp.bfloat16)
    own_values = projected_rows[:, query_width + HD :].astype(jnp.bfloat16)
    return (queries, own_keys, own_values)


def partial_softmax(queries, key_rows, value_rows, item_lengths):
    scores = jnp.einsum(
        "igd,isd->igs", queries, key_rows, preferred_element_type=jnp.float32
    ) * HD ** (-0.5)
    slot_index = jnp.arange(key_rows.shape[1])
    valid_mask = slot_index[None, None, :] < item_lengths[:, None, None]
    scores = jnp.where(valid_mask, scores, -1e30)
    peak_score = jnp.max(scores, -1)
    weights = jnp.where(valid_mask, jnp.exp(scores - peak_score[..., None]), 0.0)
    weighted = jnp.einsum("igs,isd->igd", weights, value_rows.astype(jnp.float32))
    return (peak_score, jnp.sum(weights, -1), weighted.reshape(queries.shape[0], -1))


def combine(peaks, totals, weighted, own_score, own_values):
    item_count, source_count, group_size = peaks.shape
    top_score = jnp.maximum(jnp.max(peaks, 1), own_score)
    factor = jnp.exp(peaks - top_score[:, None])
    own_weight = jnp.exp(own_score - top_score)
    denominator = jnp.sum(totals * factor, 1) + own_weight
    numerator = jnp.sum(
        weighted.reshape(item_count, source_count, group_size, HD) * factor[..., None], 1
    )
    numerator = numerator + own_weight[..., None] * own_values.astype(jnp.float32)[:, None, :]
    return (
        (numerator / denominator[..., None])
        .reshape(item_count, group_size * HD)
        .astype(jnp.bfloat16)
    )


def per_device(
    hidden_in,
    key_cache,
    value_cache,
    positions,
    query_pos,
    lengths,
    query_weight,
    key_weight,
    value_weight,
    out_weight,
    gate_weight,
    up_weight,
    down_weight,
):
    pool_index = lax.axis_index("pool")
    pool_size = lax.axis_size("pool")
    local_heads = key_cache.shape[1]
    group_size = HEADS // KV_HEADS
    query_width = group_size * HD
    all_items = PROMPTS * local_heads
    my_count = all_items // pool_size
    my_start = pool_index * my_count
    seq_local = key_cache.shape[2]
    block_cols = D // pool_size
    normed = normalize(hidden_in.astype(jnp.float32)).astype(jnp.bfloat16)
    normed_cols = lax.dynamic_slice_in_dim(normed, pool_index * block_cols, block_cols, 1)
    term = jnp.concatenate(
        [
            jnp.dot(normed_cols, query_weight, preferred_element_type=jnp.float32).reshape(
                PROMPTS, local_heads, query_width
            ),
            jnp.dot(normed_cols, key_weight, preferred_element_type=jnp.float32).reshape(
                PROMPTS, local_heads, HD
            ),
            jnp.dot(normed_cols, value_weight, preferred_element_type=jnp.float32).reshape(
                PROMPTS, local_heads, HD
            ),
        ],
        2,
    ).reshape(all_items, query_width + 2 * HD)
    cos_table, sin_table = angle_tables(positions)
    rotated = rotate(key_cache.astype(jnp.float32), cos_table[:, None], sin_table[:, None]).astype(
        jnp.bfloat16
    )
    rotated = rotated.reshape(all_items, seq_local, HD)
    value_rows = value_cache.reshape(all_items, seq_local, HD)
    item_lengths = jnp.repeat(lengths, local_heads)
    projected = sum_at_owner(term, "pool", 0)
    queries, own_keys, own_values = prepare(
        projected, my_start + jnp.arange(my_count), local_heads, query_pos
    )
    my_keys, my_values = sent_together((rotated, value_rows), "pool", 0, 1, 2)
    my_lengths = lax.dynamic_slice_in_dim(item_lengths, my_start, my_count, 0)
    peak_score, totals, weighted = partial_softmax(queries, my_keys, my_values, my_lengths)
    peaks, totals, weighted = (peak_score[:, None], totals[:, None], weighted[:, None])
    own_score = jnp.einsum(
        "igd,id->ig", queries, own_keys, preferred_element_type=jnp.float32
    ) * HD ** (-0.5)
    attended = combine(peaks, totals, weighted, own_score, own_values)
    gathered = gather_directly(attended, "pool", 0).reshape(PROMPTS, local_heads * query_width)
    attn_out = taken_together(
        jnp.dot(gathered, out_weight, preferred_element_type=jnp.float32), "heads"
    )
    hidden_cols = lax.dynamic_slice_in_dim(hidden_in, pool_index * block_cols, block_cols, 1)
    mid_state = (hidden_cols.astype(jnp.float32) + attn_out).astype(jnp.bfloat16)
    whole_state = gather_directly(mid_state, "pool", 1)
    widened = whole_state.astype(jnp.float32)
    inverse = lax.rsqrt(jnp.mean(widened * widened, -1) + EPS)
    normed_state = (whole_state.astype(jnp.float32) * inverse[:, None]).astype(jnp.bfloat16)
    gate_values = jnp.dot(normed_state, gate_weight, preferred_element_type=jnp.float32)
    up_values = jnp.dot(normed_state, up_weight, preferred_element_type=jnp.float32)
    active = (jax.nn.silu(gate_values) * up_values).astype(jnp.bfloat16)
    partial_out = jnp.dot(active, down_weight, preferred_element_type=jnp.float32)
    mlp_cols = sent_and_summed(partial_out.astype(jnp.bfloat16), "pool", 1)
    mlp_cols = taken_together(mlp_cols, "heads")
    return (mid_state.astype(jnp.float32) + mlp_cols).astype(jnp.bfloat16)


def solution(mesh):
    in_specs = (
        P("groups", None),
        P("groups", "heads", "pool", None),
        P("groups", "heads", "pool", None),
        P(None, "groups", "pool"),
        P(None, "groups"),
        P("groups"),
        P("pool", "heads"),
        P("pool", "heads"),
        P("pool", "heads"),
        P("heads", "pool"),
        P(None, ("pool", "heads")),
        P(None, ("pool", "heads")),
        P(("pool", "heads"), None),
    )
    out_specs = P("groups", "pool")
    return jax.shard_map(
        per_device, mesh=mesh, in_specs=in_specs, out_specs=out_specs, check_vma=False
    )
```

profile of v0, /device:TPU:33, one launch (start us, length us, event | category | flops | bytes accessed | tf_op | source)
XLA Modules:
  0.0 267.5 jit_solution(14200865849557301987)
XLA Ops:
  0.0 1.9 convert_element_type.134
  1.9 1.2 multiply_reduce_fusion
  3.2 1.1 fusion.53
  4.3 1.1 fusion.49
  5.4 2.3 fusion.51
  7.6 1.3 concatenate.58
  10.0 29.6 %all-to-all-start = ((f32[64,1,1280]{2,1,0:T(1,128)}), f32[64,1,1280]{2,1,0:T(1,128)S(1)}, u32[]{:S(2)}, u32[]{:S(2)}) async-start(f32[64,1,1280]{2,1,0:T(1,128)} %pad_maximum_fusion.1), calls=%async_computation | async-start | bytes 655360 | tf_op jit(solution)/shard_map/all_to_all | solution.py:26
  39.9 4.5 %fusion.11 = (f32[16,64,64]{2,1,0:T(8,128)S(1)}, f32[16,64,64]{2,1,0:T(8,128)S(1)}) fusion(f32[64]{0:T(128)S(1)} %multiply_exponential_fusion, s32[16,64]{1,0:T(8,128)S(1)} %get-tuple-element.24, s32[16,64]{1,0:T(8,128)S(1)} %get-tuple-element.25, s32[16,64]{1,0:T(8,128)S(1)} %get-tuple-element.23, pred[64]{0:T(512)(128)(4,1)S(1)} %get-tuple-element.35, ...), kind=kLoop, calls=%fused_computation.26 | loop fusion | flops 262144 | bytes 536960 | tf_op jit(solution)/shard_map/cos | solution.py:84
  45.6 2.3 pad_maximum_fusion
  47.9 11.5 %all-to-all-done = f32[64,1,1280]{2,1,0:T(1,128)S(1)} async-done(((f32[64,1,1280]{2,1,0:T(1,128)}), f32[64,1,1280]{2,1,0:T(1,128)S(1)}, u32[]{:S(2)}, u32[]{:S(2)}) %all-to-all-start) | async-done | bytes 327712 | tf_op jit(solution)/shard_map/all_to_all | solution.py:26
  59.4 10.1 %all-to-all-start.1 = ((bf16[64,64,256]{2,1,0:T(8,128)(2,1)}), bf16[64,64,256]{2,1,0:T(8,128)(2,1)}, u32[]{:S(2)}, u32[]{:S(2)}) async-start(bf16[64,64,256]{2,1,0:T(8,128)(2,1)} %pad_maximum_fusion), calls=%async_computation.1 | async-start | bytes 4194304 | tf_op jit(solution)/shard_map/all_to_all | solution.py:38
  71.2 1.9 fusion.37
  74.0 1.9 convert_bitcast_fusion.2
  76.1 86.5 %all-to-all-done.1 = bf16[64,64,256]{2,1,0:T(8,128)(2,1)} async-done(((bf16[64,64,256]{2,1,0:T(8,128)(2,1)}), bf16[64,64,256]{2,1,0:T(8,128)(2,1)}, u32[]{:S(2)}, u32[]{:S(2)}) %all-to-all-start.1) | async-done | bytes 2097184 | tf_op jit(solution)/shard_map/all_to_all | solution.py:38
  162.6 1.8 fusion.48
  164.9 1.5 fusion.6
  167.1 1.4 reduce.10
  168.6 25.7 %all_to_all.42 = bf16[64,2,512]{2,1,0:T(2,128)(2,1)S(1)} all-to-all(bf16[64,2,512]{2,1,0:T(2,128)(2,1)S(1)} %reshape.349), channel_id=1, replica_groups=mesh['groups'=2,'pool'=64,'heads'=2] {'pool'}, dimensions={0} | all-to-all | bytes 262144 | tf_op jit(solution)/shard_map/all_to_all | solution.py:53
  195.5 6.9 %all_to_all.43 = f32[2,16,128]{2,1,0:T(8,128)S(1)} all-to-all(f32[2,16,128]{2,1,0:T(8,128)S(1)} %broadcast_in_dim.167), channel_id=1, replica_groups=mesh['groups'=2,'pool'=64,'heads'=2] {'heads'}, dimensions={0} | all-to-all | bytes 32768 | tf_op jit(solution)/shard_map/all_to_all | solution.py:53
  203.1 24.9 %all_to_all.44 = bf16[64,16,128]{2,1,0:T(8,128)(2,1)S(1)} all-to-all(bf16[64,16,128]{2,1,0:T(8,128)(2,1)S(1)} %broadcast_in_dim.168), channel_id=1, replica_groups=mesh['groups'=2,'pool'=64,'heads'=2] {'pool'}, dimensions={0} | all-to-all | bytes 524288 | tf_op jit(solution)/shard_map/all_to_all | solution.py:53
  228.2 2.2 fusion.43
  230.4 3.1 %fusion.1 = bf16[2,64,8,128]{3,2,1,0:T(8,128)(2,1)S(1)} fusion(bf16[116,8192]{1,0:T(8,128)(2,1)S(1)} %copy-done, bf16[8192,116]{0,1:T(8,128)(2,1)} %param.24, f32[16,116]{1,0:T(8,128)S(1)} %fusion.43, f32[16]{0:T(128)S(1)} %add_rsqrt_fusion, bf16[64,16,128]{2,1,0:T(8,128)(2,1)S(1)} %all_to_all.44), kind=kOutput, calls=%fused_computation.6 | convolution fusion | flops 61352832 | bytes 4332864 | tf_op jit(solution)/shard_map/dot_general | solution.py:222
  233.6 24.7 %all_to_all.45 = bf16[64,16,128]{2,1,0:T(8,128)(2,1)S(1)} all-to-all(bf16[64,16,128]{2,1,0:T(8,128)(2,1)S(1)} %bitcast.98), channel_id=1, replica_groups=mesh['groups'=2,'pool'=64,'heads'=2] {'pool'}, dimensions={0} | all-to-all | bytes 524288 | tf_op jit(solution)/shard_map/all_to_all | solution.py:68
  258.4 8.5 %all_to_all.46 = f32[2,16,128]{2,1,0:T(8,128)S(1)} all-to-all(f32[2,16,128]{2,1,0:T(8,128)S(1)} %broadcast_in_dim.169), channel_id=1, replica_groups=mesh['groups'=2,'pool'=64,'heads'=2] {'heads'}, dimensions={0} | all-to-all | bytes 32768 | tf_op jit(solution)/shard_map/all_to_all | solution.py:53
  (56 shorter events, 9.3 us)
Async XLA Ops:
  0.0 230.4 %copy-start = (bf16[116,8192]{1,0:T(8,128)(2,1)S(1)}, bf16[116,8192]{1,0:T(8,128)(2,1)}, u32[]{:S(2)}) copy-start(bf16[116,8192]{1,0:T(8,128)(2,1)} %param.25) | copy-start | bytes 5701636
  1.9 37.6 %copy-start.1 = (bf16[16,4,64,128]{3,2,1,0:T(8,128)(2,1)S(1)}, bf16[16,4,64,128]{3,2,1,0:T(8,128)(2,1)}, u32[]{:S(2)}) copy-start(bf16[16,4,64,128]{3,2,1,0:T(8,128)(2,1)} %param.14) | copy-start | bytes 3145732
  8.9 30.9 %copy-start.4 = (s32[3,16,64]{2,1,0:T(8,128)S(1)}, s32[3,16,64]{2,1,0:T(8,128)}, u32[]{:S(2)}) copy-start(s32[3,16,64]{2,1,0:T(8,128)} %param.16) | copy-start | bytes 36868
  10.0 49.4 %all-to-all-start = ((f32[64,1,1280]{2,1,0:T(1,128)}), f32[64,1,1280]{2,1,0:T(1,128)S(1)}, u32[]{:S(2)}, u32[]{:S(2)}) async-start(f32[64,1,1280]{2,1,0:T(1,128)} %pad_maximum_fusion.1), calls=%async_computation | async-start | bytes 655360 | tf_op jit(solution)/shard_map/all_to_all | solution.py:26
  44.4 1.2 copy-start.2
  47.9 21.6 %copy-start.6 = (s32[16]{0:T(128)S(1)}, s32[16]{0:T(128)}, u32[]{:S(2)}) copy-start(s32[16]{0:T(128)} %param.18) | copy-start | bytes 196
  47.9 21.8 %copy-start.5 = (s32[3,16]{1,0:T(4,128)S(1)}, s32[3,16]{1,0:T(4,128)}, u32[]{:S(2)}) copy-start(s32[3,16]{1,0:T(4,128)} %param.17) | copy-start | bytes 580
  59.4 103.2 %all-to-all-start.1 = ((bf16[64,64,256]{2,1,0:T(8,128)(2,1)}), bf16[64,64,256]{2,1,0:T(8,128)(2,1)}, u32[]{:S(2)}, u32[]{:S(2)}) async-start(bf16[64,64,256]{2,1,0:T(8,128)(2,1)} %pad_maximum_fusion), calls=%async_computation.1 | async-start | bytes 4194304 | tf_op jit(solution)/shard_map/all_to_all | solution.py:38
  164.3 31.0 %copy-start.3 = (bf16[4096,128]{1,0:T(8,128)(2,1)S(1)}, bf16[4096,128]{1,0:T(8,128)(2,1)}, u32[]{:S(2)}) copy-start(bf16[4096,128]{1,0:T(8,128)(2,1)} %param.22) | copy-start | bytes 3145732
where the time goes:
time: 268 us; the launch traced here: 267 us
  waiting for transfers between devices  98 us (37%)
  blocking collectives  90.7 us (34%)
  starting transfers between devices  39.7 us (15%)
  other arithmetic  20.9 us (8%)
  matrix products  13.5 us (5%)
  local copies, waits for them, and re-layouts  4.49 us (2%)
    all_to_all x1, waiting for transfers between devices, sent_together(): lax.all_to_all(both, axis, split_axis=split_dim, concat_axis=concat_dim,...  86.5 us
    all_to_all x4, blocking collectives, copy_for_each(): lax.all_to_all(jnp.broadcast_to(value[None], (size, *value.shape)), axis,...  66 us
    all_to_all x1, starting transfers between devices, sum_at_owner(): pieces = lax.all_to_all(split_up(value, dim, size), axis, 0, 0, tiled=True)  29.6 us
    all_to_all x1, blocking collectives, sent_and_summed(): lax.all_to_all(pieces, axis, split_axis=0, concat_axis=0, tiled=True)  24.7 us
    all_to_all x1, waiting for transfers between devices, sum_at_owner(): pieces = lax.all_to_all(split_up(value, dim, size), axis, 0, 0, tiled=True)  11.5 us
    all_to_all x1, starting transfers between devices, sent_together(): lax.all_to_all(both, axis, split_axis=split_dim, concat_axis=concat_dim,...  10.1 us
  transfers between devices with their start and end apart: 2, of which 2 were waited for; matrix products, arithmetic and copies ran while one was open for 5% of the time, Pallas kernels for 0%

commit v1 on v0

v1 whole, which is shorter than its diff:
```python
import functools
import math

import jax
import jax.numpy as jnp
from jax import lax
from jax.experimental import pallas as pl
from jax.experimental.pallas import tpu as pltpu
from jax.sharding import PartitionSpec as P

HD = 128
EPS = 1e-06
THETA = 1000000.0
NX = 4
MESH = pl.DeviceIdType.MESH
F32 = jnp.float32
BF16 = jnp.bfloat16


def far_first(pool):
    nz = pool // NX
    steps = [(a, b) for a in range(nz) for b in range(NX) if (a, b) != (0, 0)]
    return sorted(steps, key=lambda s: -(min(s[0], nz - s[0]) + min(s[1], NX - s[1])))


def rotate(values, cos_table, sin_table):
    return values * cos_table + pltpu.roll(values, HD // 2, values.ndim - 1) * sin_table


def choose_ids(lane, t, h, w):
    column = lane % (HD // 2)
    first_end = HD // 8
    second_end = first_end + 3 * HD // 16
    return jnp.where(column < first_end, t, jnp.where(column < second_end, h, w))


def inverse_row(lane):
    column = (lane % (HD // 2)).astype(F32)
    return jnp.exp(column * (-2.0 * math.log(THETA) / HD))


def body(
    cfg,
    query_pos,
    lengths,
    hidden_hbm,
    key_hbm,
    value_hbm,
    positions,
    qw_hbm,
    kw_hbm,
    vw_hbm,
    ow_hbm,
    gw_hbm,
    uw_hbm,
    dw_hbm,
    out_ref,
    hidden,
    keys,
    values,
    qw,
    kw,
    vw,
    ow,
    gw,
    uw,
    dw,
    term,
    term_in,
    item,
    item_in,
    q_send,
    q_all,
    pos_t,
    o_send,
    o_in,
    lse_send,
    lse_in,
    lse_t,
    att_send,
    att_all,
    att_rows,
    att_lhs,
    hid_cols,
    proj,
    proj_in,
    mid_send,
    mid_all,
    normed_lhs,
    down,
    down_in,
    down_send,
    part_in,
    fin,
    load_sem,
    send_sem,
    recv_sem,
):
    prompts, pool, kv, group, slots = cfg
    nz = pool // NX
    group_i = lax.axis_index("groups")
    me = lax.axis_index("pool")
    core = lax.axis_index("heads")
    z = me // NX
    x = me % NX
    half = prompts // 2
    steps = far_first(pool)

    def at(dz, dx):
        return lax.rem(z + dz, nz) * NX + lax.rem(x + dx, NX)

    def dev(p):
        return (group_i, p, core)

    other = (group_i, me, 1 - core)

    loads = []
    for n, (src, dst) in enumerate(
        [
            (hidden_hbm, hidden),
            (qw_hbm, qw),
            (kw_hbm, kw),
            (vw_hbm, vw),
            (key_hbm, keys),
            (value_hbm, values),
            (ow_hbm, ow),
            (gw_hbm, gw),
            (uw_hbm, uw),
            (dw_hbm, dw),
        ]
    ):
        copy = pltpu.make_async_copy(src, dst, load_sem.at[n])
        copy.start()
        loads.append(copy)

    barrier = pltpu.get_barrier_semaphore()
    for dz, dx in steps:
        pl.semaphore_signal(barrier, inc=1, device_id=dev(at(dz, dx)), device_id_type=MESH)
    pl.semaphore_signal(barrier, inc=1, device_id=other, device_id_type=MESH)

    def send(src, dst, n, device):
        pltpu.make_async_remote_copy(
            src_ref=src,
            dst_ref=dst,
            send_sem=send_sem.at[n],
            recv_sem=recv_sem.at[n],
            device_id=device,
            device_id_type=MESH,
        ).start()

    def arrived(view, n):
        pltpu.make_async_copy(view, view, recv_sem.at[n]).wait()

    def sent(view, n):
        pltpu.make_async_copy(view, view, send_sem.at[n]).wait()

    loads[0].wait()
    wide = hidden[...].astype(F32)
    scale = lax.rsqrt(jnp.mean(wide * wide, -1, keepdims=True) + EPS)
    mine = hidden[:, pl.ds(pl.multiple_of(me * HD, HD), HD)].astype(F32)
    hid_cols[...] = mine
    normed_cols = (mine * scale).astype(BF16)
    for n in (1, 2, 3):
        loads[n].wait()
    width = group * HD
    for dx in (2, 1, 3, 0):
        g = lax.rem(x + dx, NX)
        part = jnp.dot(
            normed_cols,
            qw[:, pl.ds(pl.multiple_of(g * width, width), width)],
            preferred_element_type=F32,
        )
        for j in range(group):
            term[g, j] = part[:, j * HD : (j + 1) * HD]
        columns = pl.ds(pl.multiple_of(g * HD, HD), HD)
        term[g, group] = jnp.dot(normed_cols, kw[:, columns], preferred_element_type=F32)
        term[g, group + 1] = jnp.dot(normed_cols, vw[:, columns], preferred_element_type=F32)

    pl.semaphore_wait(barrier, pool)

    for dx in (2, 1, 3):
        g = lax.rem(x + dx, NX)
        send(term.at[g], term_in.at[dx - 1], 0, dev(at(0, dx)))

    wide_pos = jnp.concatenate(
        [positions[k].astype(F32) for k in range(3)]
        + [jnp.zeros((HD - 3 * prompts, slots), F32)],
        0,
    )
    wide_pos = jnp.concatenate([wide_pos, jnp.zeros((HD, HD - slots), F32)], 1)
    pos_t[...] = wide_pos.T

    arrived(term_in, 0)
    for j in range(group + 2):
        item[:, j, :] = term[x, j] + term_in[0, j] + term_in[1, j] + term_in[2, j]

    for dz in sorted(range(1, nz), key=lambda d: -min(d, nz - d)):
        p = lax.rem(z + dz, nz)
        send(item.at[p], item_in.at[dz - 1], 1, dev(at(dz, 0)))

    loads[4].wait()
    lane = lax.broadcasted_iota(jnp.int32, (slots, HD), 1)
    inv = inverse_row(lane)
    sign = jnp.where(lane < HD // 2, -1.0, 1.0)

    for p in range(prompts):
        ids = choose_ids(
            lane,
            pos_t[0:slots, p : p + 1],
            pos_t[0:slots, prompts + p : prompts + p + 1],
            pos_t[0:slots, 2 * prompts + p : 2 * prompts + p + 1],
        )
        angles = ids * inv
        cos_table = jnp.cos(angles)
        sin_table = jnp.sin(angles) * sign
        for g in range(kv):
            keys[p, g] = rotate(keys[p, g].astype(F32), cos_table, sin_table).astype(BF16)

    arrived(item_in, 1)
    total = item[z]
    for d in range(nz - 1):
        total = total + item_in[d]

    row = lax.broadcasted_iota(jnp.int32, (1, HD), 1)
    ids = choose_ids(
        row,
        query_pos[0, z].astype(F32),
        query_pos[1, z].astype(F32),
        query_pos[2, z].astype(F32),
    )
    angles = ids * inverse_row(row)
    cos_row = jnp.cos(angles)
    sin_row = jnp.sin(angles) * jnp.where(row < HD // 2, -1.0, 1.0)
    my_queries = rotate(total[0:group], cos_row, sin_row).astype(BF16)
    my_key = rotate(total[group : group + 1], cos_row, sin_row).astype(BF16).astype(F32)
    my_value = total[group + 1 : group + 2].astype(BF16).astype(F32)

    q_send[...] = my_queries
    for dz, dx in steps:
        send(q_send, q_all.at[me], 2, dev(at(dz, dx)))
    q_all[me] = my_queries
    loads[5].wait()
    arrived(q_all.at[pl.ds(0, pool - 1)], 2)

    rows = kv * group
    r_i = lax.broadcasted_iota(jnp.int32, (rows, kv * slots), 0)
    c_i = lax.broadcasted_iota(jnp.int32, (rows, kv * slots), 1)
    diagonal = r_i // group == c_i // slots
    slot = c_i % slots + me * slots
    eye = lax.broadcasted_iota(jnp.int32, (rows, HD), 0) == lax.broadcasted_iota(
        jnp.int32, (rows, HD), 1
    )
    for dz in sorted(range(nz), key=lambda d: -min(d, nz - d)):
        p = lax.rem(z + dz, nz)
        first = p * kv
        q4 = q_all[pl.ds(first, kv)].astype(F32).reshape(rows, HD).astype(BF16)
        k4 = keys[p].reshape(kv * slots, HD)
        v4 = values[p].reshape(kv * slots, HD)
        scores = lax.dot_general(
            q4, k4, (((1,), (1,)), ((), ())), preferred_element_type=F32
        ) * HD ** (-0.5)
        valid = diagonal & (slot < lengths[p])
        scores = jnp.where(valid, scores, -1e30)
        peak = jnp.max(scores, -1, keepdims=True)
        weights = jnp.where(valid, jnp.exp(scores - peak), 0.0).astype(BF16)
        norm = jnp.sum(weights.astype(F32), -1, keepdims=True)
        some = norm > 0.0
        lse = jnp.where(some, peak + jnp.log(jnp.where(some, norm, 1.0)), -1e30)
        blended = jnp.dot(weights, v4, preferred_element_type=F32)
        blended = blended / jnp.where(some, norm, 1.0)
        o_send[pl.ds(first, kv)] = blended.reshape(kv, group, HD).astype(BF16)
        lse_send[p] = jnp.sum(jnp.where(eye, lse, 0.0), 0, keepdims=True)
        for dx in (2, 1, 3, 0):
            if dz == 0 and dx == 0:
                continue
            to = at(dz, dx)
            slot_there = dz * NX + dx - 1
            send(lse_send.at[p], lse_in.at[slot_there], 3, dev(to))
            send(o_send.at[to], o_in.at[slot_there], 4, dev(to))

    own_score = jnp.sum(my_queries.astype(F32) * my_key, -1, keepdims=True) * HD ** (-0.5)

    o_in[pool - 1] = o_send[me]
    lse_in[pool - 1] = lse_send[z]
    arrived(lse_in.at[pl.ds(0, pool - 1)], 3)
    lse_rows = lse_in[...].reshape(pool, HD)
    lse_t[...] = jnp.concatenate([lse_rows, jnp.full((HD - pool, HD), -1e30, F32)], 0).T
    lse = lse_t[pl.ds(pl.multiple_of(x * group, group), group), :]
    top = jnp.maximum(jnp.max(lse, -1, keepdims=True), own_score)
    factor = jnp.exp(lse - top)
    own_weight = jnp.exp(own_score - top)
    denominator = jnp.sum(factor, -1, keepdims=True) + own_weight
    factor = factor / denominator
    own_weight = own_weight / denominator
    arrived(o_in.at[pl.ds(0, pool - 1)], 4)
    mixed = [own_weight * my_value, None, None, None]
    for s in range(pool):
        piece = factor[:, s : s + 1] * o_in[s].astype(F32)
        k = s % 4
        mixed[k] = piece if mixed[k] is None else mixed[k] + piece
    attended = ((mixed[0] + mixed[1]) + (mixed[2] + mixed[3])).astype(BF16)

    att_send[...] = attended
    for dz, dx in steps:
        send(att_send, att_all.at[me], 5, dev(at(dz, dx)))
    att_all[me] = attended
    loads[6].wait()
    arrived(att_all.at[pl.ds(0, pool - 1)], 5)
    att_rows[...] = att_all[...].astype(F32).reshape(pool * group, HD)
    for j in range(rows):
        att_lhs[:, j * HD : (j + 1) * HD] = att_rows[
            pl.ds(j, prompts, stride=rows), :
        ].astype(BF16)
    projected = jnp.dot(att_lhs[...], ow[...], preferred_element_type=F32)

    proj[0] = projected[0:half]
    proj[1] = projected[half:prompts]
    send(proj.at[1 - core], proj_in, 6, other)
    arrived(proj_in, 6)
    mid = (
        hid_cols[pl.ds(pl.multiple_of(core * half, half), half), :] + proj[core] + proj_in[...]
    ).astype(BF16)

    mid_send[...] = mid
    for dz, dx in steps:
        send(mid_send, mid_all.at[core, me], 7, dev(at(dz, dx)))
    mid_all[core, me] = mid
    arrived(mid_all.at[0, pl.ds(0, pool - 1)], 7)
    send(mid_all.at[core], mid_all.at[core], 8, other)
    arrived(mid_all.at[0], 8)

    inverse = []
    for c in range(2):
        state = mid_all[c].astype(F32)
        squares = jnp.sum(jnp.sum(state * state, 0), -1, keepdims=True)
        inverse.append(lax.rsqrt(squares * (1.0 / (pool * HD)) + EPS))
    for k in range(pool):
        chunk = jnp.concatenate([mid_all[c, k].astype(F32) * inverse[c] for c in range(2)], 0)
        normed_lhs[:, k * HD : (k + 1) * HD] = chunk.astype(BF16)
    loads[7].wait()
    loads[8].wait()
    gate = jnp.dot(normed_lhs[...], gw[...], preferred_element_type=F32)
    up = jnp.dot(normed_lhs[...], uw[...], preferred_element_type=F32)
    active = (gate / (1.0 + jnp.exp(-gate)) * up).astype(BF16)

    loads[9].wait()
    wide_cols = 8 * HD
    for c in range(pool // 8):
        part = jnp.dot(
            active, dw[:, c * wide_cols : (c + 1) * wide_cols], preferred_element_type=F32
        )
        for k in range(8):
            down[0, c * 8 + k] = part[0:half, k * HD : (k + 1) * HD]
            down[1, c * 8 + k] = part[half:prompts, k * HD : (k + 1) * HD]
    send(down.at[1 - core], down_in, 9, other)
    arrived(down_in, 9)
    down_send[...] = (down[core] + down_in[...]).astype(BF16)
    for dz, dx in steps:
        to = at(dz, dx)
        send(down_send.at[to], part_in.at[dz * NX + dx - 1], 10, dev(to))
    part_in[pool - 1] = down_send[me]
    arrived(part_in.at[pl.ds(0, pool - 1)], 10)
    done = mid.astype(F32) + jnp.sum(part_in[...].astype(F32), 0)
    fin[core] = done.astype(BF16)
    send(fin.at[core], fin.at[core], 11, other)
    arrived(fin.at[0], 11)
    out_ref[...] = jnp.concatenate([fin[0].astype(F32), fin[1].astype(F32)], 0).astype(BF16)

    sent(term_in, 0)
    sent(item_in, 1)
    sent(q_all.at[pl.ds(0, pool - 1)], 2)
    sent(lse_in.at[pl.ds(0, pool - 1)], 3)
    sent(o_in.at[pl.ds(0, pool - 1)], 4)
    sent(att_all.at[pl.ds(0, pool - 1)], 5)
    sent(proj_in, 6)
    sent(mid_all.at[0, pl.ds(0, pool - 1)], 7)
    sent(mid_all.at[0], 8)
    sent(down_in, 9)
    sent(part_in.at[pl.ds(0, pool - 1)], 10)
    sent(fin.at[0], 11)


def solution(mesh):
    pool = mesh.shape["pool"]

    def per_device(
        hidden_in,
        key_cache,
        value_cache,
        positions,
        query_pos,
        lengths,
        query_weight,
        key_weight,
        value_weight,
        out_weight,
        gate_weight,
        up_weight,
        down_weight,
    ):
        prompts, kv, slots, _ = key_cache.shape
        group = query_weight.shape[1] // (kv * HD)
        nz = pool // NX
        parts = group + 2
        half = prompts // 2
        hbm = pl.BlockSpec(memory_space=pltpu.HBM)
        vmem = pl.BlockSpec(memory_space=pltpu.VMEM)
        smem = pl.BlockSpec(memory_space=pltpu.SMEM)

        def like(a):
            return pltpu.VMEM(a.shape, a.dtype)

        scratch = [
            like(hidden_in),
            like(key_cache),
            like(value_cache),
            like(query_weight),
            like(key_weight),
            like(value_weight),
            like(out_weight),
            like(gate_weight),
            like(up_weight),
            like(down_weight),
            pltpu.VMEM((kv, parts, prompts, HD), F32),
            pltpu.VMEM((NX - 1, parts, prompts, HD), F32),
            pltpu.VMEM((prompts, parts, HD), F32),
            pltpu.VMEM((nz - 1, parts, HD), F32),
            pltpu.VMEM((group, HD), BF16),
            pltpu.VMEM((pool, group, HD), BF16),
            pltpu.VMEM((HD, HD), F32),
            pltpu.VMEM((pool, group, HD), BF16),
            pltpu.VMEM((pool, group, HD), BF16),
            pltpu.VMEM((prompts, 1, HD), F32),
            pltpu.VMEM((pool, 1, HD), F32),
            pltpu.VMEM((HD, HD), F32),
            pltpu.VMEM((group, HD), BF16),
            pltpu.VMEM((pool, group, HD), BF16),
            pltpu.VMEM((pool * group, HD), F32),
            pltpu.VMEM((prompts, kv * group * HD), BF16),
            pltpu.VMEM((prompts, HD), F32),
            pltpu.VMEM((2, half, HD), F32),
            pltpu.VMEM((half, HD), F32),
            pltpu.VMEM((half, HD), BF16),
            pltpu.VMEM((2, pool, half, HD), BF16),
            pltpu.VMEM((prompts, pool * HD), BF16),
            pltpu.VMEM((2, pool, half, HD), F32),
            pltpu.VMEM((pool, half, HD), F32),
            pltpu.VMEM((pool, half, HD), BF16),
            pltpu.VMEM((pool, half, HD), BF16),
            pltpu.VMEM((2, half, HD), BF16),
            pltpu.SemaphoreType.DMA((10,)),
            pltpu.SemaphoreType.DMA((12,)),
            pltpu.SemaphoreType.DMA((12,)),
        ]
        return pl.pallas_call(
            functools.partial(body, (prompts, pool, kv, group, slots)),
            out_shape=jax.ShapeDtypeStruct((prompts, HD), BF16),
            in_specs=[smem, smem, hbm, hbm, hbm, vmem] + [hbm] * 7,
            out_specs=vmem,
            scratch_shapes=scratch,
            compiler_params=pltpu.CompilerParams(
                collective_id=0, has_side_effects=True, vmem_limit_bytes=60 * 1024 * 1024
            ),
        )(
            query_pos,
            lengths,
            hidden_in,
            key_cache,
            value_cache,
            positions,
            query_weight,
            key_weight,
            value_weight,
            out_weight,
            gate_weight,
            up_weight,
            down_weight,
        )

    in_specs = (
        P("groups", None),
        P("groups", "heads", "pool", None),
        P("groups", "heads", "pool", None),
        P(None, "groups", "pool"),
        P(None, "groups"),
        P("groups"),
        P("pool", "heads"),
        P("pool", "heads"),
        P("pool", "heads"),
        P("heads", "pool"),
        P(None, ("pool", "heads")),
        P(None, ("pool", "heads")),
        P(("pool", "heads"), None),
    )
    return jax.shard_map(
        per_device, mesh=mesh, in_specs=in_specs, out_specs=P("groups", "pool"), check_vma=False
    )
```

time: 268 us -> 107 us (0.40)
  Pallas kernels: 0 us -> 99 us
  waiting for transfers between devices: 98 us -> 0 us
  blocking collectives: 90.7 us -> 0 us
  starting transfers between devices: 39.7 us -> 0 us
  other arithmetic: 20.9 us -> 0 us
  matrix products: 13.5 us -> 0 us
  local copies, waits for them, and re-layouts: 4.49 us -> 8.02 us
    pallas_call x0 -> x1, Pallas kernels: none -> 99 us  [per_device(): pl.pallas_call(functools.partial(body, (prompts, pool, kv, group, slots))...]
    all_to_all x2 -> x0, waiting for transfers between devices: 98 us -> none  [the longest x1 86.5 us: sent_together(): lax.all_to_all(both, axis, split_axis=split_dim, concat_axis=concat_dim,...]
    all_to_all x5 -> x0, blocking collectives: 90.7 us -> none  [the longest x4 66 us: copy_for_each(): lax.all_to_all(jnp.broadcast_to(value[None], (size, *value.shape)), axis,...]
    all_to_all x2 -> x0, starting transfers between devices: 39.7 us -> none  [the longest x1 29.6 us: sum_at_owner(): pieces = lax.all_to_all(split_up(value, dim, size), axis, 0, 0, tiled=True)]
    dot_general x9 -> x0, matrix products: 13.5 us -> none  [the longest x1 3.09 us: per_device(): jnp.dot(active, down_weight, preferred_element_type=jnp.float32)]
    unnamed x16 -> x5, local copies, waits for them, and re-layouts: 0.56 us -> 8.02 us
    concatenate x4 -> x0, other arithmetic: 5.35 us -> none  [the longest x1 2.29 us: sent_together(): both = jnp.concatenate(arrays, axis=along)]
    cos x1 -> x0, other arithmetic: 4.54 us -> none  [angle_tables(): return (jnp.cos(angles), jnp.sin(angles))]
  transfers between devices with their start and end apart: 2 -> 0, of which waited for: 2 -> 0; matrix products, arithmetic and copies ran while one was open for 5% -> 0% of each run, Pallas kernels for 0% -> 0%
where the time goes in v1:
time: 107 us
  Pallas kernels  99 us (93%)
  local copies, waits for them, and re-layouts  8.02 us (7%)
    pallas_call x1, Pallas kernels, per_device(): pl.pallas_call(functools.partial(body, (prompts, pool, kv, group, slots))...  99 us
    unnamed x5, local copies, waits for them, and re-layouts  8.02 us

profile of v1, /device:TPU:33, one launch (start us, length us, event | category | flops | bytes accessed | tf_op | source)
XLA Modules:
  0.0 107.0 jit_solution(17056772589307725064)
XLA Ops:
  0.0 0.0 copy-start
  0.0 4.2 %copy.14.gw_hbm = bf16[8192,116]{1,0:T(8,128)(2,1)} copy(bf16[8192,116]{0,1:T(8,128)(2,1)} %param.23) | data formatting | bytes 3801088 | tf_op args[10]
  4.2 0.0 copy-done
  4.2 2.5 %copy.15.uw_hbm = bf16[8192,116]{1,0:T(8,128)(2,1)} copy(bf16[8192,116]{0,1:T(8,128)(2,1)S(1)} %copy-done) | data formatting | bytes 3801088 | tf_op args[11]
  6.8 99.0 %shard_map.127 = bf16[16,128]{1,0:T(8,128)(2,1)} custom-call(s32[3,16]{1,0:T(4,128)} %query_pos.1, s32[16]{0:T(128)} %lengths.1, bf16[16,8192]{1,0:T(8,128)(2,1)} %hidden_hbm.1, bf16[16,4,64,128]{3,2,1,0:T(8,128)(2,1)} %key_hbm.1, bf16[16,4,64,128]{3,2,1,0:T(8,128)(2,1)} %value_hbm.1, s32[3,16,64]{2,1,0:T(8,128)} %positions.1, bf16[128,4096]{1,0:T(8,128)(2,1)} %qw_hbm.1, ...), custom_call_target="tpu_custom_call" | custom-call | tf_op jit(solution)/shard_map/pallas_call | solution.py:455
  105.8 1.3 %copy.17 = bf16[16,128]{1,0:T(8,128)(2,1)} copy(bf16[16,128]{1,0:T(8,128)(2,1)} %shard_map.127) | data formatting | bytes 8192
Async XLA Ops:
  0.0 4.2 %copy-start = (bf16[8192,116]{0,1:T(8,128)(2,1)S(1)}, bf16[8192,116]{0,1:T(8,128)(2,1)}, u32[]{:S(2)}) copy-start(bf16[8192,116]{0,1:T(8,128)(2,1)} %param.24) | copy-start | bytes 5701636

commit v2 on v1

--- a/solution.py
+++ b/solution.py
@@ -95,6 +95,7 @@
     load_sem,
     send_sem,
     recv_sem,
+    here_sem,
 ):
     prompts, pool, kv, group, slots = cfg
     nz = pool // NX
@@ -113,6 +114,15 @@
         return (group_i, p, core)
 
     other = (group_i, me, 1 - core)
+
+    barrier = pltpu.get_barrier_semaphore()
+    near = [dev(at(0, dx)) for dx in (2, 1, 3)] + [dev(at(1, 0)), dev(at(nz - 1, 0)), other]
+    for device in near:
+        pl.semaphore_signal(barrier, inc=1, device_id=device, device_id_type=MESH)
+
+    def tell(distance, n):
+        for dz in (distance, nz - distance):
+            pl.semaphore_signal(here_sem.at[n], inc=1, device_id=dev(at(dz, 0)), device_id_type=MESH)
 
     loads = []
     for n, (src, dst) in enumerate(
@@ -133,10 +143,6 @@
         copy.start()
         loads.append(copy)
 
-    barrier = pltpu.get_barrier_semaphore()
-    for dz, dx in steps:
-        pl.semaphore_signal(barrier, inc=1, device_id=dev(at(dz, dx)), device_id_type=MESH)
-    pl.semaphore_signal(barrier, inc=1, device_id=other, device_id_type=MESH)
 
     def send(src, dst, n, device):
         pltpu.make_async_remote_copy(
@@ -155,6 +161,8 @@
         pltpu.make_async_copy(view, view, send_sem.at[n]).wait()
 
     loads[0].wait()
+    pl.semaphore_wait(barrier, len(near))
+    tell(1, 0)
     wide = hidden[...].astype(F32)
     scale = lax.rsqrt(jnp.mean(wide * wide, -1, keepdims=True) + EPS)
     mine = hidden[:, pl.ds(pl.multiple_of(me * HD, HD), HD)].astype(F32)
@@ -175,12 +183,13 @@
         columns = pl.ds(pl.multiple_of(g * HD, HD), HD)
         term[g, group] = jnp.dot(normed_cols, kw[:, columns], preferred_element_type=F32)
         term[g, group + 1] = jnp.dot(normed_cols, vw[:, columns], preferred_element_type=F32)
-
-    pl.semaphore_wait(barrier, pool)
-
-    for dx in (2, 1, 3):
-        g = lax.rem(x + dx, NX)
-        send(term.at[g], term_in.at[dx - 1], 0, dev(at(0, dx)))
+        if dx:
+            send(term.at[g], term_in.at[dx - 1], 0, dev(at(0, dx)))
+
+    pl.semaphore_wait(here_sem.at[0], 2)
+    tell(2, 1)
+    pl.semaphore_wait(here_sem.at[1], 2)
+    tell(4, 2)
 
     wide_pos = jnp.concatenate(
         [positions[k].astype(F32) for k in range(3)]
@@ -194,6 +203,7 @@
     for j in range(group + 2):
         item[:, j, :] = term[x, j] + term_in[0, j] + term_in[1, j] + term_in[2, j]
 
+    pl.semaphore_wait(here_sem.at[2], 2)
     for dz in sorted(range(1, nz), key=lambda d: -min(d, nz - d)):
         p = lax.rem(z + dz, nz)
         send(item.at[p], item_in.at[dz - 1], 1, dev(at(dz, 0)))
@@ -339,8 +349,9 @@
         normed_lhs[:, k * HD : (k + 1) * HD] = chunk.astype(BF16)
     loads[7].wait()
     loads[8].wait()
-    gate = jnp.dot(normed_lhs[...], gw[...], preferred_element_type=F32)
-    up = jnp.dot(normed_lhs[...], uw[...], preferred_element_type=F32)
+    across = (((1,), (1,)), ((), ()))
+    gate = lax.dot_general(normed_lhs[...], gw[...], across, preferred_element_type=F32)
+    up = lax.dot_general(normed_lhs[...], uw[...], across, preferred_element_type=F32)
     active = (gate / (1.0 + jnp.exp(-gate)) * up).astype(BF16)
 
     loads[9].wait()
@@ -398,6 +409,7 @@
         up_weight,
         down_weight,
     ):
+        gate_weight, up_weight = gate_weight.T, up_weight.T
         prompts, kv, slots, _ = key_cache.shape
         group = query_weight.shape[1] // (kv * HD)
         nz = pool // NX
@@ -451,6 +463,7 @@
             pltpu.SemaphoreType.DMA((10,)),
             pltpu.SemaphoreType.DMA((12,)),
             pltpu.SemaphoreType.DMA((12,)),
+            pltpu.SemaphoreType.REGULAR((3,)),
         ]
         return pl.pallas_call(
             functools.partial(body, (prompts, pool, kv, group, slots)),

time: 107 us -> 95.7 us (0.89)
  local copies, waits for them, and re-layouts: 8.02 us -> 1.28 us
  Pallas kernels: 99 us -> 94.2 us
    unnamed x5 -> x1, local copies, waits for them, and re-layouts: 8.02 us -> 1.28 us
    pallas_call x1, Pallas kernels: 99 us -> 94.2 us  [per_device(): pl.pallas_call(functools.partial(body, (prompts, pool, kv, group, slots))...]
where the time goes in v2:
time: 95.7 us; the launch traced here: 95.5 us
  Pallas kernels  94.2 us (98%)
  local copies, waits for them, and re-layouts  1.28 us (1%)
    pallas_call x1, Pallas kernels, per_device(): pl.pallas_call(functools.partial(body, (prompts, pool, kv, group, slots))...  94.2 us

profile of v2, /device:TPU:33, one launch (start us, length us, event | category | flops | bytes accessed | tf_op | source)
XLA Modules:
  0.0 95.5 jit_solution(11223151012899617354)
XLA Ops:
  0.0 94.2 %shard_map.127 = bf16[16,128]{1,0:T(8,128)(2,1)} custom-call(s32[3,16]{1,0:T(4,128)} %query_pos.1, s32[16]{0:T(128)} %lengths.1, bf16[16,8192]{1,0:T(8,128)(2,1)} %hidden_hbm.1, bf16[16,4,64,128]{3,2,1,0:T(8,128)(2,1)} %key_hbm.1, bf16[16,4,64,128]{3,2,1,0:T(8,128)(2,1)} %value_hbm.1, s32[3,16,64]{2,1,0:T(8,128)} %positions.1, bf16[128,4096]{1,0:T(8,128)(2,1)} %qw_hbm.1, ...), custom_call_target="tpu_custom_call" | custom-call | tf_op jit(solution)/shard_map/pallas_call | solution.py:468
  94.2 1.3 %copy.15 = bf16[16,128]{1,0:T(8,128)(2,1)} copy(bf16[16,128]{1,0:T(8,128)(2,1)} %shard_map.127) | data formatting | bytes 8192

commit v3 on v2

--- a/solution.py
+++ b/solution.py
@@ -76,8 +76,7 @@
     o_in,
     lse_send,
     lse_in,
-    lse_t,
-    att_send,
+    join,
     att_all,
     att_rows,
     att_lhs,
@@ -96,6 +95,8 @@
     send_sem,
     recv_sem,
     here_sem,
+    q_sem,
+    down_sem,
 ):
     prompts, pool, kv, group, slots = cfg
     nz = pool // NX
@@ -144,18 +145,18 @@
         loads.append(copy)
 
 
-    def send(src, dst, n, device):
+    def send(src, dst, n, device, arrival=None):
         pltpu.make_async_remote_copy(
             src_ref=src,
             dst_ref=dst,
             send_sem=send_sem.at[n],
-            recv_sem=recv_sem.at[n],
+            recv_sem=recv_sem.at[n] if arrival is None else arrival,
             device_id=device,
             device_id_type=MESH,
         ).start()
 
-    def arrived(view, n):
-        pltpu.make_async_copy(view, view, recv_sem.at[n]).wait()
+    def arrived(view, n, arrival=None):
+        pltpu.make_async_copy(view, view, recv_sem.at[n] if arrival is None else arrival).wait()
 
     def sent(view, n):
         pltpu.make_async_copy(view, view, send_sem.at[n]).wait()
@@ -247,75 +248,107 @@
 
     q_send[...] = my_queries
     for dz, dx in steps:
-        send(q_send, q_all.at[me], 2, dev(at(dz, dx)))
+        send(q_send, q_all.at[me], 2, dev(at(dz, dx)), q_sem.at[dz])
     q_all[me] = my_queries
     loads[5].wait()
-    arrived(q_all.at[pl.ds(0, pool - 1)], 2)
 
     rows = kv * group
     r_i = lax.broadcasted_iota(jnp.int32, (rows, kv * slots), 0)
     c_i = lax.broadcasted_iota(jnp.int32, (rows, kv * slots), 1)
     diagonal = r_i // group == c_i // slots
     slot = c_i % slots + me * slots
-    eye = lax.broadcasted_iota(jnp.int32, (rows, HD), 0) == lax.broadcasted_iota(
-        jnp.int32, (rows, HD), 1
+    lane_minus_row = lax.broadcasted_iota(jnp.int32, (rows, HD), 1) - lax.broadcasted_iota(
+        jnp.int32, (rows, HD), 0
     )
-    for dz in sorted(range(nz), key=lambda d: -min(d, nz - d)):
-        p = lax.rem(z + dz, nz)
+    mine_here = lax.broadcasted_iota(jnp.int32, (rows, 1), 0) // group == x
+
+    def part_of(p, own):
         first = p * kv
-        q4 = q_all[pl.ds(first, kv)].astype(F32).reshape(rows, HD).astype(BF16)
+        q4 = q_all[pl.ds(first, kv)].astype(F32).reshape(rows, HD)
         k4 = keys[p].reshape(kv * slots, HD)
         v4 = values[p].reshape(kv * slots, HD)
         scores = lax.dot_general(
-            q4, k4, (((1,), (1,)), ((), ())), preferred_element_type=F32
+            q4.astype(BF16), k4, (((1,), (1,)), ((), ())), preferred_element_type=F32
         ) * HD ** (-0.5)
         valid = diagonal & (slot < lengths[p])
         scores = jnp.where(valid, scores, -1e30)
         peak = jnp.max(scores, -1, keepdims=True)
+        if own:
+            own_score = jnp.sum(q4 * my_key[0], -1, keepdims=True) * HD ** (-0.5)
+            peak = jnp.where(mine_here, jnp.maximum(peak, own_score), peak)
         weights = jnp.where(valid, jnp.exp(scores - peak), 0.0).astype(BF16)
         norm = jnp.sum(weights.astype(F32), -1, keepdims=True)
+        blended = jnp.dot(weights, v4, preferred_element_type=F32)
+        if own:
+            own_weight = jnp.where(mine_here, jnp.exp(jnp.minimum(own_score - peak, 0.0)), 0.0)
+            norm = norm + own_weight
+            blended = blended + own_weight * my_value[0]
         some = norm > 0.0
-        lse = jnp.where(some, peak + jnp.log(jnp.where(some, norm, 1.0)), -1e30)
-        blended = jnp.dot(weights, v4, preferred_element_type=F32)
-        blended = blended / jnp.where(some, norm, 1.0)
-        o_send[pl.ds(first, kv)] = blended.reshape(kv, group, HD).astype(BF16)
-        lse_send[p] = jnp.sum(jnp.where(eye, lse, 0.0), 0, keepdims=True)
-        for dx in (2, 1, 3, 0):
-            if dz == 0 and dx == 0:
-                continue
-            to = at(dz, dx)
-            slot_there = dz * NX + dx - 1
-            send(lse_send.at[p], lse_in.at[slot_there], 3, dev(to))
-            send(o_send.at[to], o_in.at[slot_there], 4, dev(to))
-
-    own_score = jnp.sum(my_queries.astype(F32) * my_key, -1, keepdims=True) * HD ** (-0.5)
-
-    o_in[pool - 1] = o_send[me]
-    lse_in[pool - 1] = lse_send[z]
-    arrived(lse_in.at[pl.ds(0, pool - 1)], 3)
-    lse_rows = lse_in[...].reshape(pool, HD)
-    lse_t[...] = jnp.concatenate([lse_rows, jnp.full((HD - pool, HD), -1e30, F32)], 0).T
-    lse = lse_t[pl.ds(pl.multiple_of(x * group, group), group), :]
-    top = jnp.maximum(jnp.max(lse, -1, keepdims=True), own_score)
+        safe = jnp.where(some, norm, 1.0)
+        lse = jnp.where(some, peak + jnp.log(safe), -1e30)
+        blended = blended / safe
+        o_send[p] = blended.reshape(kv, group, HD).astype(BF16)
+        eye_lse = jnp.where(lane_minus_row == 0, lse, 0.0)
+        lse_send[p] = jnp.sum(eye_lse, 0, keepdims=True)
+
+    for near in range(nz // 2 + 1):
+        away = sorted({near, (nz - near) % nz})
+        for dz in away:
+            count = NX - 1 if dz == 0 else NX
+            arrived(q_all.at[pl.ds(0, count)], 2, q_sem.at[dz])
+        for dz in away:
+            part_of(lax.rem(z - dz + nz, nz), dz == 0)
+        for dz in away:
+            p = lax.rem(z - dz + nz, nz)
+            if dz != nz // 2:
+                owner = dev(at(nz - dz + nz // 2, 0))
+                send(lse_send.at[p], lse_in.at[z], 3, owner)
+                send(o_send.at[p], o_in.at[z], 4, owner)
+
+    theirs = lax.rem(z + nz // 2, nz)
+    o_in[z] = o_send[theirs]
+    lse_in[z] = lse_send[theirs]
+    arrived(lse_in.at[pl.ds(0, nz - 1)], 3)
+    lse_rows = jnp.concatenate(
+        [lse_in[...].reshape(nz, HD), jnp.full((HD - nz, HD), -1e30, F32)], 0
+    )
+    lse = lse_rows.T[0:rows]
+    top = jnp.max(lse, -1, keepdims=True)
     factor = jnp.exp(lse - top)
-    own_weight = jnp.exp(own_score - top)
-    denominator = jnp.sum(factor, -1, keepdims=True) + own_weight
-    factor = factor / denominator
-    own_weight = own_weight / denominator
-    arrived(o_in.at[pl.ds(0, pool - 1)], 4)
-    mixed = [own_weight * my_value, None, None, None]
-    for s in range(pool):
-        piece = factor[:, s : s + 1] * o_in[s].astype(F32)
-        k = s % 4
+    norm = jnp.sum(factor, -1, keepdims=True)
+    factor = factor / norm
+    joined_lse = top + jnp.log(norm)
+    arrived(o_in.at[pl.ds(0, nz - 1)], 4)
+    mixed = [None, None]
+    for s in range(nz):
+        piece = factor[:, s : s + 1] * o_in[s].astype(F32).reshape(rows, HD)
+        k = s % 2
         mixed[k] = piece if mixed[k] is None else mixed[k] + piece
-    attended = ((mixed[0] + mixed[1]) + (mixed[2] + mixed[3])).astype(BF16)
-
-    att_send[...] = attended
-    for dz, dx in steps:
-        send(att_send, att_all.at[me], 5, dev(at(dz, dx)))
-    att_all[me] = attended
+    join[x, 0:kv] = (mixed[0] + mixed[1]).reshape(kv, group, HD)
+    head_lane = lax.broadcasted_iota(jnp.int32, (group, HD), 1)
+    packed = jnp.zeros((group, HD), F32)
+    for g in range(kv):
+        packed = jnp.where(head_lane == g, joined_lse[g * group : (g + 1) * group], packed)
+    join[x, kv] = packed
+
+    for dx in (2, 1, 3):
+        send(join.at[x], join.at[x], 5, dev(at(0, dx)))
+    arrived(join.at[pl.ds(0, NX - 1)], 5)
+    attended = []
+    for g in range(kv):
+        lse = [join[n, kv][:, g : g + 1] for n in range(NX)]
+        top = jnp.maximum(jnp.maximum(lse[0], lse[1]), jnp.maximum(lse[2], lse[3]))
+        factor = [jnp.exp(v - top) for v in lse]
+        norm = (factor[0] + factor[1]) + (factor[2] + factor[3])
+        total = sum(factor[n] * join[n, g] for n in range(NX)) / norm
+        attended.append(total.astype(BF16))
+
+    for g in range(kv):
+        att_all[theirs, g] = attended[g]
+    for dz in sorted(range(1, nz), key=lambda d: -min(d, nz - d)):
+        send(att_all.at[theirs], att_all.at[theirs], 12, dev(at(dz, 0)))
     loads[6].wait()
-    arrived(att_all.at[pl.ds(0, pool - 1)], 5)
+    arrived(att_all.at[pl.ds(0, nz - 1)], 12)
     att_rows[...] = att_all[...].astype(F32).reshape(pool * group, HD)
     for j in range(rows):
         att_lhs[:, j * HD : (j + 1) * HD] = att_rows[
@@ -355,21 +388,42 @@
     active = (gate / (1.0 + jnp.exp(-gate)) * up).astype(BF16)
 
     loads[9].wait()
-    wide_cols = 8 * HD
-    for c in range(pool // 8):
-        part = jnp.dot(
-            active, dw[:, c * wide_cols : (c + 1) * wide_cols], preferred_element_type=F32
-        )
-        for k in range(8):
-            down[0, c * 8 + k] = part[0:half, k * HD : (k + 1) * HD]
-            down[1, c * 8 + k] = part[half:prompts, k * HD : (k + 1) * HD]
-    send(down.at[1 - core], down_in, 9, other)
-    arrived(down_in, 9)
-    down_send[...] = (down[core] + down_in[...]).astype(BF16)
-    for dz, dx in steps:
-        to = at(dz, dx)
-        send(down_send.at[to], part_in.at[dz * NX + dx - 1], 10, dev(to))
-    part_in[pool - 1] = down_send[me]
+    order = sorted(range(nz), key=lambda d: -min(d, nz - d))
+
+    def down_columns(n):
+        for dz in order[n * NX : (n + 1) * NX]:
+            first = lax.rem(z + dz, nz) * NX
+            part = jnp.dot(
+                active,
+                dw[:, pl.ds(pl.multiple_of(first * HD, NX * HD), NX * HD)],
+                preferred_element_type=F32,
+            )
+            at_n = (n * NX + order[n * NX : (n + 1) * NX].index(dz)) * NX
+            for k in range(NX):
+                down[0, at_n + k] = part[0:half, k * HD : (k + 1) * HD]
+                down[1, at_n + k] = part[half:prompts, k * HD : (k + 1) * HD]
+        block = pl.ds(n * NX * NX, NX * NX)
+        send(down.at[1 - core, block], down_in.at[block], 9, other, down_sem.at[n])
+
+    def down_out(n):
+        block = pl.ds(n * NX * NX, NX * NX)
+        arrived(down_in.at[block], 9, down_sem.at[n])
+        down_send[block] = (down[core, block] + down_in[block]).astype(BF16)
+        for i, dz in enumerate(order[n * NX : (n + 1) * NX]):
+            for dx in (2, 1, 3, 0):
+                if dz == 0 and dx == 0:
+                    continue
+                entry = (n * NX + i) * NX + lax.rem(x + dx, NX)
+                send(down_send.at[entry], part_in.at[dz * NX + dx - 1], 10, dev(at(dz, dx)))
+
+    down_columns(0)
+    down_columns(1)
+    for n in range(2, nz // NX):
+        down_out(n - 2)
+        down_columns(n)
+    down_out(nz // NX - 2)
+    down_out(nz // NX - 1)
+    part_in[pool - 1] = down_send[(nz - 1) * NX + x]
     arrived(part_in.at[pl.ds(0, pool - 1)], 10)
     done = mid.astype(F32) + jnp.sum(part_in[...].astype(F32), 0)
     fin[core] = done.astype(BF16)
@@ -380,9 +434,10 @@
     sent(term_in, 0)
     sent(item_in, 1)
     sent(q_all.at[pl.ds(0, pool - 1)], 2)
-    sent(lse_in.at[pl.ds(0, pool - 1)], 3)
-    sent(o_in.at[pl.ds(0, pool - 1)], 4)
-    sent(att_all.at[pl.ds(0, pool - 1)], 5)
+    sent(lse_in.at[pl.ds(0, nz - 1)], 3)
+    sent(o_in.at[pl.ds(0, nz - 1)], 4)
+    sent(join.at[pl.ds(0, NX - 1)], 5)
+    sent(att_all.at[pl.ds(0, nz - 1)], 12)
     sent(proj_in, 6)
     sent(mid_all.at[0, pl.ds(0, pool - 1)], 7)
     sent(mid_all.at[0], 8)
@@ -440,13 +495,12 @@
             pltpu.VMEM((group, HD), BF16),
             pltpu.VMEM((pool, group, HD), BF16),
             pltpu.VMEM((HD, HD), F32),
-            pltpu.VMEM((pool, group, HD), BF16),
-            pltpu.VMEM((pool, group, HD), BF16),
+            pltpu.VMEM((prompts, kv, group, HD), BF16),
+            pltpu.VMEM((nz, kv, group, HD), BF16),
             pltpu.VMEM((prompts, 1, HD), F32),
-            pltpu.VMEM((pool, 1, HD), F32),
-            pltpu.VMEM((HD, HD), F32),
-            pltpu.VMEM((group, HD), BF16),
-            pltpu.VMEM((pool, group, HD), BF16),
+            pltpu.VMEM((nz, 1, HD), F32),
+            pltpu.VMEM((NX, kv + 1, group, HD), F32),
+            pltpu.VMEM((prompts, kv, group, HD), BF16),
             pltpu.VMEM((pool * group, HD), F32),
             pltpu.VMEM((prompts, kv * group * HD), BF16),
             pltpu.VMEM((prompts, HD), F32),
@@ -461,9 +515,11 @@
             pltpu.VMEM((pool, half, HD), BF16),
             pltpu.VMEM((2, half, HD), BF16),
             pltpu.SemaphoreType.DMA((10,)),
-            pltpu.SemaphoreType.DMA((12,)),
-            pltpu.SemaphoreType.DMA((12,)),
+            pltpu.SemaphoreType.DMA((13,)),
+            pltpu.SemaphoreType.DMA((13,)),
             pltpu.SemaphoreType.REGULAR((3,)),
+            pltpu.SemaphoreType.DMA((nz,)),
+            pltpu.SemaphoreType.DMA((nz // NX,)),
         ]
         return pl.pallas_call(
             functools.partial(body, (prompts, pool, kv, group, slots)),

time: 95.7 us -> 94 us (0.982)
  Pallas kernels: 94.2 us -> 92.5 us
    pallas_call x1, Pallas kernels: 94.2 us -> 92.5 us  [per_device(): pl.pallas_call(functools.partial(body, (prompts, pool, kv, group, slots))...]
where the time goes in v3:
time: 94 us; the launch traced here: 93.8 us
  Pallas kernels  92.5 us (98%)
  local copies, waits for them, and re-layouts  1.28 us (1%)
    pallas_call x1, Pallas kernels, per_device(): pl.pallas_call(functools.partial(body, (prompts, pool, kv, group, slots))...  92.5 us

profile of v3, /device:TPU:33, one launch (start us, length us, event | category | flops | bytes accessed | tf_op | source)
XLA Modules:
  0.0 93.8 jit_solution(11672931630091184893)
XLA Ops:
  0.0 92.5 %shard_map.127 = bf16[16,128]{1,0:T(8,128)(2,1)} custom-call(s32[3,16]{1,0:T(4,128)} %query_pos.1, s32[16]{0:T(128)} %lengths.1, bf16[16,8192]{1,0:T(8,128)(2,1)} %hidden_hbm.1, bf16[16,4,64,128]{3,2,1,0:T(8,128)(2,1)} %key_hbm.1, bf16[16,4,64,128]{3,2,1,0:T(8,128)(2,1)} %value_hbm.1, s32[3,16,64]{2,1,0:T(8,128)} %positions.1, bf16[128,4096]{1,0:T(8,128)(2,1)} %qw_hbm.1, ...), custom_call_target="tpu_custom_call" | custom-call | tf_op jit(solution)/shard_map/pallas_call | solution.py:524
  92.5 1.3 %copy.15 = bf16[16,128]{1,0:T(8,128)(2,1)} copy(bf16[16,128]{1,0:T(8,128)(2,1)} %shard_map.127) | data formatting | bytes 8192

commit v4 on v3

--- a/solution.py
+++ b/solution.py
@@ -11,6 +11,7 @@
 HD = 128
 EPS = 1e-06
 THETA = 1000000.0
+LAG = 6
 NX = 4
 MESH = pl.DeviceIdType.MESH
 F32 = jnp.float32
@@ -41,12 +42,12 @@
 
 def body(
     cfg,
-    query_pos,
-    lengths,
+    query_pos_hbm,
+    lengths_hbm,
     hidden_hbm,
     key_hbm,
     value_hbm,
-    positions,
+    positions_hbm,
     qw_hbm,
     kw_hbm,
     vw_hbm,
@@ -55,6 +56,9 @@
     uw_hbm,
     dw_hbm,
     out_ref,
+    query_pos,
+    lengths,
+    positions,
     hidden,
     keys,
     values,
@@ -97,6 +101,7 @@
     here_sem,
     q_sem,
     down_sem,
+    q_x_sem,
 ):
     prompts, pool, kv, group, slots = cfg
     nz = pool // NX
@@ -115,15 +120,6 @@
         return (group_i, p, core)
 
     other = (group_i, me, 1 - core)
-
-    barrier = pltpu.get_barrier_semaphore()
-    near = [dev(at(0, dx)) for dx in (2, 1, 3)] + [dev(at(1, 0)), dev(at(nz - 1, 0)), other]
-    for device in near:
-        pl.semaphore_signal(barrier, inc=1, device_id=device, device_id_type=MESH)
-
-    def tell(distance, n):
-        for dz in (distance, nz - distance):
-            pl.semaphore_signal(here_sem.at[n], inc=1, device_id=dev(at(dz, 0)), device_id_type=MESH)
 
     loads = []
     for n, (src, dst) in enumerate(
@@ -138,12 +134,28 @@
             (gw_hbm, gw),
             (uw_hbm, uw),
             (dw_hbm, dw),
+            (positions_hbm, positions),
+            (query_pos_hbm, query_pos),
+            (lengths_hbm, lengths),
         ]
     ):
         copy = pltpu.make_async_copy(src, dst, load_sem.at[n])
-        copy.start()
         loads.append(copy)
-
+    for n in (0, 1, 2, 3):
+        loads[n].start()
+
+
+    barrier = pltpu.get_barrier_semaphore()
+    near = [dev(at(0, dx)) for dx in (2, 1, 3)] + [dev(at(1, 0)), dev(at(nz - 1, 0)), other]
+    for device in near:
+        pl.semaphore_signal(barrier, inc=1, device_id=device, device_id_type=MESH)
+
+    def tell(distance, n):
+        for dz in (distance, nz - distance):
+            pl.semaphore_signal(here_sem.at[n], inc=1, device_id=dev(at(dz, 0)), device_id_type=MESH)
+
+    for n in (10, 11, 12, 4, 5, 6, 7, 8, 9):
+        loads[n].start()
 
     def send(src, dst, n, device, arrival=None):
         pltpu.make_async_remote_copy(
@@ -192,6 +204,8 @@
     pl.semaphore_wait(here_sem.at[1], 2)
     tell(4, 2)
 
+    for n in (10, 11, 12):
+        loads[n].wait()
     wide_pos = jnp.concatenate(
         [positions[k].astype(F32) for k in range(3)]
         + [jnp.zeros((HD - 3 * prompts, slots), F32)],
@@ -247,9 +261,9 @@
     my_value = total[group + 1 : group + 2].astype(BF16).astype(F32)
 
     q_send[...] = my_queries
-    for dz, dx in steps:
-        send(q_send, q_all.at[me], 2, dev(at(dz, dx)), q_sem.at[dz])
     q_all[me] = my_queries
+    for dz in sorted(range(1, nz), key=lambda d: -min(d, nz - d)):
+        send(q_send, q_all.at[me], 2, dev(at(dz, 0)), q_sem.at[dz])
     loads[5].wait()
 
     rows = kv * group
@@ -291,11 +305,21 @@
         eye_lse = jnp.where(lane_minus_row == 0, lse, 0.0)
         lse_send[p] = jnp.sum(eye_lse, 0, keepdims=True)
 
-    for near in range(nz // 2 + 1):
-        away = sorted({near, (nz - near) % nz})
+    def away_at(near):
+        return sorted({near, (nz - near) % nz})
+
+    def relay(near):
+        for dz in away_at(near):
+            entry = lax.rem(z - dz + nz, nz) * kv + x
+            if dz:
+                arrived(q_all.at[pl.ds(0, 1)], 2, q_sem.at[dz])
+            for dx in (2, 1, 3):
+                send(q_all.at[entry], q_all.at[entry], 13, dev(at(0, dx)), q_x_sem.at[dz])
+
+    def attend(near):
+        away = away_at(near)
         for dz in away:
-            count = NX - 1 if dz == 0 else NX
-            arrived(q_all.at[pl.ds(0, count)], 2, q_sem.at[dz])
+            arrived(q_all.at[pl.ds(0, NX - 1)], 13, q_x_sem.at[dz])
         for dz in away:
             part_of(lax.rem(z - dz + nz, nz), dz == 0)
         for dz in away:
@@ -304,6 +328,13 @@
                 owner = dev(at(nz - dz + nz // 2, 0))
                 send(lse_send.at[p], lse_in.at[z], 3, owner)
                 send(o_send.at[p], o_in.at[z], 4, owner)
+
+    reach = nz // 2 + 1
+    for near in range(reach + LAG):
+        if near < reach:
+            relay(near)
+        if near >= LAG:
+            attend(near - LAG)
 
     theirs = lax.rem(z + nz // 2, nz)
     o_in[z] = o_send[theirs]
@@ -433,7 +464,8 @@
 
     sent(term_in, 0)
     sent(item_in, 1)
-    sent(q_all.at[pl.ds(0, pool - 1)], 2)
+    sent(q_all.at[pl.ds(0, nz - 1)], 2)
+    sent(q_all.at[pl.ds(0, nz * (NX - 1))], 13)
     sent(lse_in.at[pl.ds(0, nz - 1)], 3)
     sent(o_in.at[pl.ds(0, nz - 1)], 4)
     sent(join.at[pl.ds(0, NX - 1)], 5)
@@ -472,12 +504,14 @@
         half = prompts // 2
         hbm = pl.BlockSpec(memory_space=pltpu.HBM)
         vmem = pl.BlockSpec(memory_space=pltpu.VMEM)
-        smem = pl.BlockSpec(memory_space=pltpu.SMEM)
 
         def like(a):
             return pltpu.VMEM(a.shape, a.dtype)
 
         scratch = [
+            pltpu.SMEM(query_pos.shape, jnp.int32),
+            pltpu.SMEM(lengths.shape, jnp.int32),
+            like(positions),
             like(hidden_in),
             like(key_cache),
             like(value_cache),
@@ -514,17 +548,18 @@
             pltpu.VMEM((pool, half, HD), BF16),
             pltpu.VMEM((pool, half, HD), BF16),
             pltpu.VMEM((2, half, HD), BF16),
-            pltpu.SemaphoreType.DMA((10,)),
             pltpu.SemaphoreType.DMA((13,)),
-            pltpu.SemaphoreType.DMA((13,)),
+            pltpu.SemaphoreType.DMA((14,)),
+            pltpu.SemaphoreType.DMA((14,)),
             pltpu.SemaphoreType.REGULAR((3,)),
             pltpu.SemaphoreType.DMA((nz,)),
             pltpu.SemaphoreType.DMA((nz // NX,)),
+            pltpu.SemaphoreType.DMA((nz,)),
         ]
         return pl.pallas_call(
             functools.partial(body, (prompts, pool, kv, group, slots)),
             out_shape=jax.ShapeDtypeStruct((prompts, HD), BF16),
-            in_specs=[smem, smem, hbm, hbm, hbm, vmem] + [hbm] * 7,
+            in_specs=[hbm] * 13,
             out_specs=vmem,
             scratch_shapes=scratch,
             compiler_params=pltpu.CompilerParams(

time: 94 us -> 92.1 us (0.980)
  Pallas kernels: 92.5 us -> 90.7 us
    pallas_call x1, Pallas kernels: 92.5 us -> 90.7 us  [per_device(): pl.pallas_call(functools.partial(body, (prompts, pool, kv, group, slots))...]
where the time goes in v4:
time: 92.1 us; the launch traced here: 91.9 us
  Pallas kernels  90.7 us (98%)
  local copies, waits for them, and re-layouts  1.28 us (1%)
    pallas_call x1, Pallas kernels, per_device(): pl.pallas_call(functools.partial(body, (prompts, pool, kv, group, slots))...  90.7 us

profile of v4, /device:TPU:33, one launch (start us, length us, event | category | flops | bytes accessed | tf_op | source)
XLA Modules:
  0.0 91.9 jit_solution(18186103552761797430)
XLA Ops:
  0.0 90.7 %shard_map.127 = bf16[16,128]{1,0:T(8,128)(2,1)} custom-call(s32[3,16]{1,0:T(4,128)} %query_pos_hbm.1, s32[16]{0:T(128)} %lengths_hbm.1, bf16[16,8192]{1,0:T(8,128)(2,1)} %hidden_hbm.1, bf16[16,4,64,128]{3,2,1,0:T(8,128)(2,1)} %key_hbm.1, bf16[16,4,64,128]{3,2,1,0:T(8,128)(2,1)} %value_hbm.1, s32[3,16,64]{2,1,0:T(8,128)} %positions_hbm.1, ...), custom_call_target="tpu_custom_call" | custom-call | tf_op jit(solution)/shard_map/pallas_call | solution.py:559
  90.7 1.3 %copy.15 = bf16[16,128]{1,0:T(8,128)(2,1)} copy(bf16[16,128]{1,0:T(8,128)(2,1)} %shard_map.127) | data formatting | bytes 8192

commit v5 on v4

--- a/solution.py
+++ b/solution.py
@@ -241,11 +241,6 @@
         for g in range(kv):
             keys[p, g] = rotate(keys[p, g].astype(F32), cos_table, sin_table).astype(BF16)
 
-    arrived(item_in, 1)
-    total = item[z]
-    for d in range(nz - 1):
-        total = total + item_in[d]
-
     row = lax.broadcasted_iota(jnp.int32, (1, HD), 1)
     ids = choose_ids(
         row,
@@ -256,6 +251,11 @@
     angles = ids * inverse_row(row)
     cos_row = jnp.cos(angles)
     sin_row = jnp.sin(angles) * jnp.where(row < HD // 2, -1.0, 1.0)
+    arrived(item_in, 1)
+    total = item[z]
+    for d in range(nz - 1):
+        total = total + item_in[d]
+
     my_queries = rotate(total[0:group], cos_row, sin_row).astype(BF16)
     my_key = rotate(total[group : group + 1], cos_row, sin_row).astype(BF16).astype(F32)
     my_value = total[group + 1 : group + 2].astype(BF16).astype(F32)
@@ -401,13 +401,16 @@
     mid_all[core, me] = mid
     arrived(mid_all.at[0, pl.ds(0, pool - 1)], 7)
     send(mid_all.at[core], mid_all.at[core], 8, other)
+
+    def scale_of(half_of):
+        state = mid_all[half_of].astype(F32)
+        squares = jnp.sum(jnp.sum(state * state, 0), -1, keepdims=True)
+        return lax.rsqrt(squares * (1.0 / (pool * HD)) + EPS)
+
+    my_scale = scale_of(core)
     arrived(mid_all.at[0], 8)
-
-    inverse = []
-    for c in range(2):
-        state = mid_all[c].astype(F32)
-        squares = jnp.sum(jnp.sum(state * state, 0), -1, keepdims=True)
-        inverse.append(lax.rsqrt(squares * (1.0 / (pool * HD)) + EPS))
+    their_scale = scale_of(1 - core)
+    inverse = [jnp.where(core == c, my_scale, their_scale) for c in range(2)]
     for k in range(pool):
         chunk = jnp.concatenate([mid_all[c, k].astype(F32) * inverse[c] for c in range(2)], 0)
         normed_lhs[:, k * HD : (k + 1) * HD] = chunk.astype(BF16)

time: 92.1 us -> 93.3 us (1.013)
  Pallas kernels: 90.7 us -> 91.9 us
    pallas_call x1, Pallas kernels: 90.7 us -> 91.9 us  [per_device(): pl.pallas_call(functools.partial(body, (prompts, pool, kv, group, slots))...]
where the time goes in v5:
time: 93.3 us; the launch traced here: 93.2 us
  Pallas kernels  91.9 us (98%)
  local copies, waits for them, and re-layouts  1.28 us (1%)
    pallas_call x1, Pallas kernels, per_device(): pl.pallas_call(functools.partial(body, (prompts, pool, kv, group, slots))...  91.9 us

profile of v5, /device:TPU:33, one launch (start us, length us, event | category | flops | bytes accessed | tf_op | source)
XLA Modules:
  0.0 93.2 jit_solution(17826172290094528594)
XLA Ops:
  0.0 91.9 %shard_map.127 = bf16[16,128]{1,0:T(8,128)(2,1)} custom-call(s32[3,16]{1,0:T(4,128)} %query_pos_hbm.1, s32[16]{0:T(128)} %lengths_hbm.1, bf16[16,8192]{1,0:T(8,128)(2,1)} %hidden_hbm.1, bf16[16,4,64,128]{3,2,1,0:T(8,128)(2,1)} %key_hbm.1, bf16[16,4,64,128]{3,2,1,0:T(8,128)(2,1)} %value_hbm.1, s32[3,16,64]{2,1,0:T(8,128)} %positions_hbm.1, ...), custom_call_target="tpu_custom_call" | custom-call | tf_op jit(solution)/shard_map/pallas_call | solution.py:562
  91.9 1.3 %copy.15 = bf16[16,128]{1,0:T(8,128)(2,1)} copy(bf16[16,128]{1,0:T(8,128)(2,1)} %shard_map.127) | data formatting | bytes 8192

commit v6 on v4

--- a/solution.py
+++ b/solution.py
@@ -262,7 +262,7 @@
 
     q_send[...] = my_queries
     q_all[me] = my_queries
-    for dz in sorted(range(1, nz), key=lambda d: -min(d, nz - d)):
+    for dz in sorted(range(1, nz), key=lambda d: min(d, nz - d)):
         send(q_send, q_all.at[me], 2, dev(at(dz, 0)), q_sem.at[dz])
     loads[5].wait()
 

time: 92.1 us -> 92.6 us (level)
  no operation moved by 1% of the time
where the time goes in v6:
time: 92.6 us; the launch traced here: 92.5 us
  Pallas kernels  91.2 us (98%)
  local copies, waits for them, and re-layouts  1.28 us (1%)
    pallas_call x1, Pallas kernels, per_device(): pl.pallas_call(functools.partial(body, (prompts, pool, kv, group, slots))...  91.2 us

profile of v6, /device:TPU:33, one launch (start us, length us, event | category | flops | bytes accessed | tf_op | source)
XLA Modules:
  0.0 92.5 jit_solution(11218816861525164082)
XLA Ops:
  0.0 91.2 %shard_map.127 = bf16[16,128]{1,0:T(8,128)(2,1)} custom-call(s32[3,16]{1,0:T(4,128)} %query_pos_hbm.1, s32[16]{0:T(128)} %lengths_hbm.1, bf16[16,8192]{1,0:T(8,128)(2,1)} %hidden_hbm.1, bf16[16,4,64,128]{3,2,1,0:T(8,128)(2,1)} %key_hbm.1, bf16[16,4,64,128]{3,2,1,0:T(8,128)(2,1)} %value_hbm.1, s32[3,16,64]{2,1,0:T(8,128)} %positions_hbm.1, ...), custom_call_target="tpu_custom_call" | custom-call | tf_op jit(solution)/shard_map/pallas_call | solution.py:559
  91.2 1.3 %copy.15 = bf16[16,128]{1,0:T(8,128)(2,1)} copy(bf16[16,128]{1,0:T(8,128)(2,1)} %shard_map.127) | data formatting | bytes 8192
